TPU v7x, 32 devices: a whole 2x2x4 slice. The times are simulated.
32 devices in a mesh: seq: 8 (over z, y), tensor: 4 (over x, core).
Axes of the slice: x: 2, y: 2, z: 4, core: 2. Of those that a mesh axis runs over, the one named last changes fastest.
Arguments:
- layer_input: bfloat16 [2048, 4096], P('seq', 'tensor'), may hold values from -6 to 6
- norm_gain: float32 [4096], replicated, may hold values from 0.1 to 1.9
- in_weights: bfloat16 [2, 4096, 2048], P(None, None, 'tensor'), may hold values from -0.09375 to 0.09375
- conv_weight: float32 [4, 2048], P(None, 'tensor'), may hold values from -4 to 4
- conv_bias: float32 [2048], P('tensor'), may hold values from -3 to 3
- gate_weights: bfloat16 [2, 8, 256, 256], P(None, 'tensor'), may hold values from -0.375 to 0.375
- gate_bias: float32 [2, 2048], P(None, 'tensor'), may hold values from -4 to 4
- decay_rate: float32 [2048], P('tensor'), may hold values from 1e-06 to 0.03, as said below
- out_weight: bfloat16 [2048, 4096], P('tensor'), may hold values from -0.1875 to 0.1875
- mlp_gain: float32 [4096], replicated, may hold values from 0.1 to 1.9
- mlp_in: bfloat16 [2, 4096, 6144], P(None, 'seq', 'tensor'), may hold values from -0.09375 to 0.09375
- mlp_out: bfloat16 [6144, 4096], P('tensor', 'seq'), may hold values from -0.109375 to 0.109375
Outputs:
- block_output: bfloat16 [2048, 4096], P('seq', 'tensor')
Inputs may be any that keep to these rules, and one draw needn't show every extreme that they name: `decay_rate`: every rate is positive.
All inputs are finite; a program needn't handle non-finite values.
Results may differ from a plain program's by a relative error of at most 0.015.
Values may be sent and summed in bfloat16 or wider, within the bound.
A program may use at most 128 MiB of HBM per device.

v0:
```python
import jax
import jax.numpy as jnp
from jax import lax
from jax.sharding import PartitionSpec as P


def shifted(value, axis, steps):
    count = lax.axis_size(axis)
    first, last = (max(0, -steps), min(count, count - steps))
    return lax.ppermute(value, axis, [(source, source + steps) for source in range(first, last)])


def prefix(value, axis, combine, identity):
    size, here = (lax.axis_size(axis), lax.axis_index(axis))
    everything = jax.tree.map(lambda part: lax.all_gather(part, axis), value)
    start = jax.tree.map(
        lambda part, zero: jnp.broadcast_to(jnp.asarray(zero, part.dtype), part.shape),
        value,
        identity,
    )

    def hop(k, before):
        reached = k < here
        new = combine(before, jax.tree.map(lambda part: part[k], everything))
        return jax.tree.map(lambda a, b: jnp.where(reached, a, b), new, before)

    return lax.fori_loop(0, size, hop, start)


def rms_scale(rows, gain):
    values = rows.astype(jnp.float32)
    mean_square = jnp.mean(values * values, axis=-1, keepdims=True)
    return (values * lax.rsqrt(mean_square + 1e-06) * gain).astype(jnp.bfloat16)


def chain_step(earlier, later):
    return (earlier[0] * later[0], later[0] * earlier[1] + later[1])


def shards(
    layer_input,
    norm_gain,
    in_weights,
    conv_weight,
    conv_bias,
    gate_weights,
    gate_bias,
    decay_rate,
    out_weight,
    mlp_gain,
    mlp_in,
    mlp_out,
):
    whole_rows = lax.all_gather(layer_input, "tensor", axis=1, tiled=True)
    normed = rms_scale(whole_rows, norm_gain)
    branch_x = jnp.dot(normed, in_weights[0], preferred_element_type=jnp.float32).astype(
        jnp.bfloat16
    )
    branch_y = jax.nn.gelu(
        jnp.dot(normed, in_weights[1], preferred_element_type=jnp.float32), approximate=True
    )
    num_tokens = branch_x.shape[0]
    rim_rows = conv_weight.shape[0] - 1
    earlier_rows = shifted(branch_x[num_tokens - rim_rows :], "seq", 1)
    padded = jnp.concatenate([earlier_rows, branch_x], axis=0).astype(jnp.float32)
    convolved = jnp.zeros(branch_x.shape, jnp.float32) + conv_bias
    for tap_index in range(conv_weight.shape[0]):
        start_row = rim_rows - tap_index
        convolved = convolved + conv_weight[tap_index] * padded[start_row : start_row + num_tokens]
    conv_out = convolved.astype(jnp.bfloat16)
    local_blocks = gate_weights.shape[1]
    block_width = gate_weights.shape[2]
    blocks_in = conv_out.reshape(num_tokens, local_blocks, block_width)
    gate_pre = jnp.einsum(
        "tnc,knce->ktne", blocks_in, gate_weights, preferred_element_type=jnp.float32
    )
    gate_pre = gate_pre.reshape(2, num_tokens, local_blocks * block_width) + gate_bias[:, None, :]
    log_decay = -8.0 * jax.nn.sigmoid(gate_pre[0]) * decay_rate
    decay = jnp.exp(log_decay)
    driven = (
        conv_out.astype(jnp.float32)
        * jax.nn.sigmoid(gate_pre[1])
        * jnp.sqrt(-jnp.expm1(2.0 * log_decay))
    )
    cum_decay, cum_state = lax.associative_scan(chain_step, (decay, driven), axis=0)
    identity = (jnp.ones_like(cum_decay[-1]), jnp.zeros_like(cum_state[-1]))
    entering = prefix((cum_decay[-1], cum_state[-1]), "seq", chain_step, identity)
    carried = entering[1]
    state = cum_decay * carried + cum_state
    mixed = (state * branch_y).astype(jnp.bfloat16)
    partial_sums = jnp.dot(mixed, out_weight, preferred_element_type=jnp.float32)
    full_sums = lax.psum(partial_sums.astype(jnp.bfloat16), "tensor").astype(jnp.float32)
    mid_full = (whole_rows.astype(jnp.float32) + full_sums).astype(jnp.bfloat16)
    own_width = layer_input.shape[1]
    residual = lax.dynamic_slice_in_dim(
        mid_full, lax.axis_index("tensor") * own_width, own_width, 1
    )
    mlp_normed = rms_scale(mid_full, mlp_gain)
    gate_up = jnp.einsum(
        "tr,krf->ktf",
        mlp_normed,
        lax.all_gather(mlp_in, "seq", axis=1, tiled=True),
        preferred_element_type=jnp.float32,
    )
    hidden = (jax.nn.gelu(gate_up[0], approximate=True) * gate_up[1]).astype(jnp.bfloat16)
    down_terms = jnp.dot(
        hidden,
        lax.all_gather(mlp_out, "seq", axis=1, tiled=True),
        preferred_element_type=jnp.float32,
    )
    down_share = lax.psum_scatter(
        down_terms.astype(jnp.bfloat16), "tensor", scatter_dimension=1, tiled=True
    ).astype(jnp.float32)
    return (residual.astype(jnp.float32) + down_share).astype(jnp.bfloat16)


def solution(mesh):
    return jax.shard_map(
        shards,
        mesh=mesh,
        in_specs=(
            P("seq", "tensor"),
            P(),
            P(None, None, "tensor"),
            P(None, "tensor"),
            P("tensor"),
            P(None, "tensor", None, None),
            P(None, "tensor"),
            P("tensor"),
            P("tensor", None),
            P(),
            P(None, "seq", "tensor"),
            P("tensor", "seq"),
        ),
        out_specs=P("seq", "tensor"),
        check_vma=False,
    )
```

profile of v0, /device:TPU:0, one launch (start us, length us, event | category | flops | bytes accessed | tf_op | source)
XLA Modules:
  0.0 835.9 jit_solution(12491428809460878877)
XLA Ops:
  7.4 0.7 all-gather.6.cloned.1.call-update
  8.1 0.9 fusion.115
  9.0 26.0 %all-gather.6.cloned.1.call-done = bf16[256,4096]{1,0:T(8,128)(2,1)} async-done(((bf16[256,1024]{1,0:T(8,128)(2,1)}), bf16[256,4096]{1,0:T(8,128)(2,1)}) %all-gather.6.cloned.1.call-update) | async-done | bytes 2097168 | tf_op jit(solution)/shard_map/all_gather | solution.py:54
  35.0 2.1 fusion.3
  37.2 4.1 fusion.26
  41.3 3.4 collective-permute-start
  44.7 1.3 collective-permute-done
  46.8 0.6 copy.18
  47.4 0.8 reshape.41
  48.4 0.8 fusion.91
  52.4 1.4 slice.328
  53.8 1.4 slice.367
  56.2 1.7 pad.129
  58.1 2.0 add_multiply_fusion.1
  60.2 1.7 pad.128
  61.8 0.7 add_bitcast_fusion
  62.5 27.9 %all-gather.1 = f32[8,1,512]{2,1,0:T(1,128)S(1)} all-gather(f32[1,1,512]{2,1,0:T(1,128)S(1)} %add_bitcast_fusion), channel_id=1, replica_groups=mesh['seq'=8,'tensor'=4] {'seq'}, dimensions={0}, use_global_device_ids=true | all-gather | bytes 18432 | tf_op jit(solution)/shard_map/all_gather | solution.py:15
  90.4 1.6 pad.113
  92.1 1.0 pad_maximum_fusion
  93.1 1.7 pad.112
  94.7 0.7 add_bitcast_fusion.1
  95.5 26.1 %all-gather = f32[8,1,512]{2,1,0:T(1,128)S(1)} all-gather(f32[1,1,512]{2,1,0:T(1,128)S(1)} %add_bitcast_fusion.1), channel_id=1, replica_groups=mesh['seq'=8,'tensor'=4] {'seq'}, dimensions={0}, use_global_device_ids=true | all-gather | bytes 18432 | tf_op jit(solution)/shard_map/all_gather | solution.py:15
  122.0 7.9 convolution_convert_fusion.1
  130.6 0.5 all-gather.10.cloned.1.call-update
  131.4 46.4 %all-reduce.34.cloned.1.call-done = bf16[256,4096]{1,0:T(8,128)(2,1)} async-done(((bf16[256,4096]{1,0:T(8,128)(2,1)}), bf16[256,4096]{1,0:T(8,128)(2,1)}) %all-reduce.34.cloned.1.call-update) | async-done | bytes 2097168 | tf_op jit(solution)/shard_map/psum | solution.py:92
  177.8 3.9 fusion
  181.7 427.0 %all-gather.8.cloned.1.call-done = bf16[2,4096,1536]{2,1,0:T(8,128)(2,1)} async-done(((bf16[2,512,1536]{2,1,0:T(8,128)(2,1)}), bf16[2,4096,1536]{2,1,0:T(8,128)(2,1)}) %all-gather.8.cloned.1.call-update) | async-done | bytes 25165840 | tf_op jit(solution)/shard_map/all_gather | solution.py:102
  608.7 13.4 %convolution_bitcast_fusion = f32[2,256,1536]{2,1,0:T(8,128)} fusion(bf16[2,4096,1536]{2,1,0:T(8,128)(2,1)} %all-gather.8.cloned.1.call-done, bf16[256,4096]{1,0:T(8,128)(2,1)} %get-tuple-element.129, f32[4096]{0:T(1024)S(1)} %copy-done.8, f32[256]{0:T(256)S(1)} %add_rsqrt_fusion), kind=kOutput, calls=%fused_computation.23 | convolution fusion | flops 6446645248 | bytes 30426112 | tf_op jit(solution)/shard_map/tr,krf->ktf/dot_general | solution.py:99
  622.1 164.4 %all-gather.10.cloned.1.call-done = bf16[1536,4096]{1,0:T(8,128)(2,1)} async-done(((bf16[1536,512]{1,0:T(8,128)(2,1)}), bf16[1536,4096]{1,0:T(8,128)(2,1)}) %all-gather.10.cloned.1.call-update) | async-done | bytes 12582928 | tf_op jit(solution)/shard_map/all_gather | solution.py:108
  786.5 10.6 %convolution_convert_fusion = bf16[256,4096]{1,0:T(8,128)(2,1)} fusion(bf16[1536,4096]{1,0:T(8,128)(2,1)} %all-gather.10.cloned.1.call-done, f32[2,256,1536]{2,1,0:T(8,128)} %convolution_bitcast_fusion), kind=kOutput, calls=%fused_computation.8 | convolution fusion | flops 3226206208 | bytes 17825792 | tf_op jit(solution)/shard_map/dot_general | solution.py:106
  797.1 29.5 %reduce-scatter.2.cloned.1.call-done = bf16[256,1024]{1,0:T(8,128)(2,1)} async-done(((bf16[256,4096]{1,0:T(8,128)(2,1)}), bf16[256,1024]{1,0:T(8,128)(2,1)}) %reduce-scatter.2.cloned.1.call-update) | async-done | bytes 524304 | tf_op jit(solution)/shard_map/reduce_scatter | solution.py:111
  826.6 2.2 add_convert_fusion
  (168 shorter events, 6.3 us)
Async XLA Ops:
  7.4 39.1 %copy-start = (bf16[2,2,256,256]{3,2,1,0:T(8,128)(2,1)S(1)}, bf16[2,2,256,256]{3,2,1,0:T(8,128)(2,1)}, u32[]{:S(2)}) copy-start(bf16[2,2,256,256]{3,2,1,0:T(8,128)(2,1)} %param.19) | copy-start | bytes 1572868
  7.4 27.7 %all-gather.6.cloned.1.call-start = ((), (), s32[]{:S(2)}) async-start(), calls=%async_computation.1 | async-start | bytes 2621440 | tf_op jit(solution)/shard_map/all_gather | solution.py:54
  8.1 169.7 %all-reduce.34.cloned.1.call-start = ((), (), s32[]{:S(2)}) async-start(), calls=%async_computation.2 | async-start | bytes 4194304 | tf_op jit(solution)/shard_map/psum | solution.py:92
  37.1 7.6 copy-start.6
  37.1 9.0 %copy-start.4 = (f32[512]{0:T(512)S(1)}, f32[512]{0:T(512)}, u32[]{:S(2)}) copy-start(f32[512]{0:T(512)} %param.18) | copy-start | bytes 6148
  41.3 4.7 collective-permute-start
  46.4 1.8 copy-start.5
  58.1 63.9 %copy-start.2 = (bf16[256,4096]{1,0:T(8,128)(2,1)S(1)}, bf16[256,4096]{1,0:T(8,128)(2,1)}, u32[]{:S(2)}) copy-start(bf16[256,4096]{1,0:T(8,128)(2,1)} %all-gather.6.cloned.1.call-done) | copy-start | bytes 6291460
  58.1 63.9 %copy-start.7 = (f32[4096]{0:T(1024)S(1)}, f32[4096]{0:T(1024)}, u32[]{:S(2)}) copy-start(f32[4096]{0:T(1024)} %param.15) | copy-start | bytes 49156
  60.1 61.9 %copy-start.3 = (f32[256,512]{1,0:T(8,128)S(1)}, f32[256,512]{1,0:T(8,128)}, u32[]{:S(2)}) copy-start(f32[256,512]{1,0:T(8,128)} %pad.129) | copy-start | bytes 1572868
  130.0 478.7 %all-gather.8.cloned.1.call-start = ((), (), s32[]{:S(2)}) async-start(), calls=%async_computation.3 | async-start | bytes 28311552 | tf_op jit(solution)/shard_map/all_gather | solution.py:102
  130.6 656.0 %all-gather.10.cloned.1.call-start = ((), (), s32[]{:S(2)}) async-start(), calls=%async_computation.4 | async-start | bytes 14155776 | tf_op jit(solution)/shard_map/all_gather | solution.py:108
  131.2 477.6 %copy-start.8 = (f32[4096]{0:T(1024)S(1)}, f32[4096]{0:T(1024)}, u32[]{:S(2)}) copy-start(f32[4096]{0:T(1024)} %param.23) | copy-start | bytes 49156
  131.2 695.4 %reduce-scatter.2.cloned.1.call-start = ((), (), s32[]{:S(2)}) async-start(), calls=%async_computation.5 | async-start | bytes 2621440 | tf_op jit(solution)/shard_map/reduce_scatter | solution.py:111
  786.5 42.3 %copy-start.1 = (bf16[2,2,256,256]{3,2,1,0:T(8,128)(2,1)S(1)}, bf16[2,2,256,256]{3,2,1,0:T(8,128)(2,1)}, u32[]{:S(2)}) copy-start(bf16[2,2,256,256]{3,2,1,0:T(8,128)(2,1)} %param.19) | copy-start | bytes 1572868
Sparse Core Ops, SparseCore 0:
  9.7 25.2 all-gather.5
  130.1 47.6 all-reduce.33
  797.2 29.3 reduce-scatter.1
Sparse Core Ops, SparseCore 1:
  132.0 476.6 all-gather.7
  610.6 175.9 all-gather.9
where the time goes:
time: 836 us
  waiting for transfers between devices  696 us (83%)
  blocking collectives  54 us (6%)
  matrix products  36.4 us (4%)
  between operations  15.4 us (2%)
  local copies, waits for them, and re-layouts  15.1 us (2%)
  other arithmetic  14.7 us (2%)
    all_gather x1, waiting for transfers between devices, shards(): lax.all_gather(mlp_in, 'seq', axis=1, tiled=True)  427 us
    all_gather x1, waiting for transfers between devices, shards(): lax.all_gather(mlp_out, 'seq', axis=1, tiled=True)  164 us
    all_gather x2, blocking collectives, prefix(): everything = jax.tree.map(lambda part: lax.all_gather(part, axis), value)  54 us
    psum x1, waiting for transfers between devices, shards(): lax.psum(partial_sums.astype(jnp.bfloat16), 'tensor').astype(jnp.float32)  46.4 us
    reduce_scatter x1, waiting for transfers between devices, shards(): lax.psum_scatter(down_terms.astype(jnp.bfloat16), 'tensor', scatter_dimen...  29.5 us
    all_gather x1, waiting for transfers between devices, shards(): whole_rows = lax.all_gather(layer_input, 'tensor', axis=1, tiled=True)  26 us
  transfers between devices with their start and end apart: 6, of which 6 were waited for; matrix products, arithmetic and copies ran while one was open for 2% of the time, Pallas kernels for 0%

commit v1 on v0

--- a/solution.py
+++ b/solution.py
@@ -2,6 +2,19 @@
 import jax.numpy as jnp
 from jax import lax
 from jax.sharding import PartitionSpec as P
+
+
+def ring_gather(x, axis, dim):
+    ways = lax.axis_size(axis)
+    up = [(d, (d + 1) % ways) for d in range(ways)]
+    down = [(d, (d - 1) % ways) for d in range(ways)]
+    earlier, later = ([x], [x])
+    for _ in range(ways // 2):
+        earlier.append(lax.ppermute(earlier[-1], axis, up))
+    for _ in range((ways - 1) // 2):
+        later.append(lax.ppermute(later[-1], axis, down))
+    line = jnp.concatenate([*earlier[::-1], *later[1:]], axis=dim)
+    return jnp.roll(line, (lax.axis_index(axis) - ways // 2) * x.shape[dim], axis=dim)
 
 
 def shifted(value, axis, steps):
@@ -97,10 +110,7 @@
     )
     mlp_normed = rms_scale(mid_full, mlp_gain)
     gate_up = jnp.einsum(
-        "tr,krf->ktf",
-        mlp_normed,
-        lax.all_gather(mlp_in, "seq", axis=1, tiled=True),
-        preferred_element_type=jnp.float32,
+        "tr,krf->ktf", mlp_normed, ring_gather(mlp_in, "seq", 1), preferred_element_type=jnp.float32
     )
     hidden = (jax.nn.gelu(gate_up[0], approximate=True) * gate_up[1]).astype(jnp.bfloat16)
     down_terms = jnp.dot(

time: 836 us -> 798 us (0.955)
  waiting for transfers between devices: 696 us -> 589 us
  local copies, waits for them, and re-layouts: 15.1 us -> 63.6 us
  starting transfers between devices: 3.72 us -> 23.7 us
    ppermute x0 -> x7, waiting for transfers between devices: none -> 531 us  [the longest x4 396 us: ring_gather(): earlier.append(lax.ppermute(earlier[-1], axis, up))]
    all_gather x1 -> x0, waiting for transfers between devices: 427 us -> none  [shards(): lax.all_gather(mlp_in, 'seq', axis=1, tiled=True)]
    all_gather x1, waiting for transfers between devices: 164 us -> 0.01 us  [shards(): lax.all_gather(mlp_out, 'seq', axis=1, tiled=True)]
    unnamed x20 -> x48, local copies, waits for them, and re-layouts: 0.05 us -> 48 us
    psum x1, waiting for transfers between devices: 46.4 us -> 0.01 us  [shards(): lax.psum(partial_sums.astype(jnp.bfloat16), 'tensor').astype(jnp.float32)]
    ppermute x0 -> x7, starting transfers between devices: none -> 20.2 us  [the longest x3 14.7 us: ring_gather(): later.append(lax.ppermute(later[-1], axis, down))]
  transfers between devices with their start and end apart: 6 -> 12, of which waited for: 6 -> 9; matrix products, arithmetic and copies ran while one was open for 2% -> 8% of each run, Pallas kernels for 0% -> 0%
where the time goes in v1:
time: 798 us; the launch traced here: 797 us
  waiting for transfers between devices  589 us (74%)
  local copies, waits for them, and re-layouts  63.6 us (8%)
  blocking collectives  54 us (7%)
  matrix products  36.7 us (5%)
  starting transfers between devices  23.7 us (3%)
  between operations  15.5 us (2%)
  other arithmetic  13.8 us (2%)
    ppermute x4, waiting for transfers between devices, ring_gather(): earlier.append(lax.ppermute(earlier[-1], axis, up))  396 us
    ppermute x3, waiting for transfers between devices, ring_gather(): later.append(lax.ppermute(later[-1], axis, down))  135 us
    all_gather x2, blocking collectives, prefix(): everything = jax.tree.map(lambda part: lax.all_gather(part, axis), value)  54 us
    unnamed x48, local copies, waits for them, and re-layouts  48 us
    reduce_scatter x1, waiting for transfers between devices, shards(): lax.psum_scatter(down_terms.astype(jnp.bfloat16), 'tensor', scatter_dimen...  29.9 us
    all_gather x1, waiting for transfers between devices, shards(): whole_rows = lax.all_gather(layer_input, 'tensor', axis=1, tiled=True)  26 us
  transfers between devices with their start and end apart: 12, of which 9 were waited for; matrix products, arithmetic and copies ran while one was open for 8% of the time, Pallas kernels for 0%

profile of v1, /device:TPU:0, one launch (start us, length us, event | category | flops | bytes accessed | tf_op | source)
XLA Modules:
  0.0 796.8 jit_solution(16321595823166893535)
XLA Ops:
  9.0 26.0 %all-gather.5.cloned.1.call-done = bf16[256,4096]{1,0:T(8,128)(2,1)} async-done(((bf16[256,1024]{1,0:T(8,128)(2,1)}), bf16[256,4096]{1,0:T(8,128)(2,1)}) %all-gather.5.cloned.1.call-update) | async-done | bytes 2097168 | tf_op jit(solution)/shard_map/all_gather | solution.py:67
  35.0 2.1 fusion.5
  37.2 4.1 fusion.31
  41.3 3.4 collective-permute-start
  60.7 27.9 %all-gather.1 = f32[8,1,512]{2,1,0:T(1,128)S(1)} all-gather(f32[1,1,512]{2,1,0:T(1,128)S(1)} %add_bitcast_fusion), channel_id=1, replica_groups=mesh['seq'=8,'tensor'=4] {'seq'}, dimensions={0}, use_global_device_ids=true | all-gather | bytes 18432 | tf_op jit(solution)/shard_map/all_gather | solution.py:28
  92.1 26.1 %all-gather = f32[8,1,512]{2,1,0:T(1,128)S(1)} all-gather(f32[1,1,512]{2,1,0:T(1,128)S(1)} %add_bitcast_fusion.1), channel_id=1, replica_groups=mesh['seq'=8,'tensor'=4] {'seq'}, dimensions={0}, use_global_device_ids=true | all-gather | bytes 18432 | tf_op jit(solution)/shard_map/all_gather | solution.py:28
  118.7 7.8 convolution_convert_fusion.1
  127.1 3.3 copy.23
  130.5 126.7 %collective-permute-done.1 = bf16[2,512,1536]{1,2,0:T(8,128)(2,1)S(1)} collective-permute-done((bf16[2,512,1536]{1,2,0:T(8,128)(2,1)S(1)}, bf16[2,512,1536]{1,2,0:T(8,128)(2,1)S(1)}, u32[]{:S(2)}, u32[]{:S(2)}) %collective-permute-start.1) | collective-permute-done | bytes 3145760 | tf_op jit(solution)/shard_map/ppermute | solution.py:13
  257.2 4.7 collective-permute-start.5
  261.9 181.8 %collective-permute-done.2 = bf16[2,512,1536]{1,2,0:T(8,128)(2,1)S(1)} collective-permute-done((bf16[2,512,1536]{1,2,0:T(8,128)(2,1)S(1)}, bf16[2,512,1536]{1,2,0:T(8,128)(2,1)S(1)}, u32[]{:S(2)}, u32[]{:S(2)}) %collective-permute-start.2) | collective-permute-done | bytes 3145760 | tf_op jit(solution)/shard_map/ppermute | solution.py:13
  443.7 2.9 collective-permute-start.3
  446.6 16.6 %collective-permute-done.5 = bf16[2,512,1536]{1,2,0:T(8,128)(2,1)S(1)} collective-permute-done((bf16[2,512,1536]{1,2,0:T(8,128)(2,1)S(1)}, bf16[2,512,1536]{1,2,0:T(8,128)(2,1)S(1)}, u32[]{:S(2)}, u32[]{:S(2)}) %collective-permute-start.5) | collective-permute-done | bytes 3145760 | tf_op jit(solution)/shard_map/ppermute | solution.py:15
  463.2 7.0 collective-permute-start.6
  470.2 87.3 %collective-permute-done.3 = bf16[2,512,1536]{1,2,0:T(8,128)(2,1)} collective-permute-done((bf16[2,512,1536]{1,2,0:T(8,128)(2,1)S(1)}, bf16[2,512,1536]{1,2,0:T(8,128)(2,1)}, u32[]{:S(2)}, u32[]{:S(2)}) %collective-permute-start.3) | collective-permute-done | bytes 3145760 | tf_op jit(solution)/shard_map/ppermute | solution.py:13
  557.5 2.6 collective-permute-start.4
  560.1 84.0 %collective-permute-done.6 = bf16[2,512,1536]{1,2,0:T(8,128)(2,1)} collective-permute-done((bf16[2,512,1536]{1,2,0:T(8,128)(2,1)S(1)}, bf16[2,512,1536]{1,2,0:T(8,128)(2,1)}, u32[]{:S(2)}, u32[]{:S(2)}) %collective-permute-start.6) | collective-permute-done | bytes 3145760 | tf_op jit(solution)/shard_map/ppermute | solution.py:15
  644.1 3.0 collective-permute-start.7
  647.1 3.2 fusion.2
  650.3 4.5 constant_dynamic-update-slice_fusion.15
  654.9 3.9 constant_dynamic-update-slice_fusion.14
  668.6 3.8 constant_dynamic-update-slice_fusion.9
  672.5 34.5 %collective-permute-done.7 = bf16[2,512,1536]{1,2,0:T(8,128)(2,1)} collective-permute-done((bf16[2,512,1536]{1,2,0:T(8,128)(2,1)}, bf16[2,512,1536]{1,2,0:T(8,128)(2,1)}, u32[]{:S(2)}, u32[]{:S(2)}) %collective-permute-start.7) | collective-permute-done | bytes 3145760 | tf_op jit(solution)/shard_map/ppermute | solution.py:15
  707.0 3.8 constant_dynamic-update-slice_fusion.8
  710.8 3.7 constant_dynamic-update-slice_fusion.7
  714.5 3.8 constant_dynamic-update-slice_fusion.6
  725.7 3.7 constant_dynamic-update-slice_fusion.1
  729.4 3.8 constant_dynamic-update-slice_fusion
  733.2 13.5 %fusion.15 = f32[2,256,1536]{1,2,0:T(8,128)} fusion(bf16[2,8192,1536]{1,2,0:T(8,128)(2,1)} %constant_dynamic-update-slice_fusion, s32[]{:T(128)S(6)} %select_n.40, bf16[256,4096]{1,0:T(8,128)(2,1)S(1)} %get-tuple-element.129, f32[4096]{0:T(1024)S(1)} %copy-done.14, f32[256]{0:T(256)S(1)} %add_rsqrt_fusion), kind=kOutput, calls=%fused_computation.25 | convolution fusion | flops 6446645248 | bytes 30426116 | tf_op jit(solution)/shard_map/tr,krf->ktf/dot_general | solution.py:112
  746.7 10.9 %convolution_convert_fusion = bf16[256,4096]{1,0:T(8,128)(2,1)} fusion(bf16[1536,4096]{1,0:T(8,128)(2,1)} %all-gather.7.cloned.1.call-done, f32[2,256,1536]{1,2,0:T(8,128)} %fusion.15), kind=kOutput, calls=%fused_computation.10 | convolution fusion | flops 3226206208 | bytes 17825792 | tf_op jit(solution)/shard_map/dot_general | solution.py:116
  757.6 29.9 %reduce-scatter.2.cloned.1.call-done = bf16[256,1024]{1,0:T(8,128)(2,1)} async-done(((bf16[256,4096]{1,0:T(8,128)(2,1)}), bf16[256,1024]{1,0:T(8,128)(2,1)}) %reduce-scatter.2.cloned.1.call-update) | async-done | bytes 524304 | tf_op jit(solution)/shard_map/reduce_scatter | solution.py:121
  787.5 2.2 add_convert_fusion
  (208 shorter events, 39.0 us)
Async XLA Ops:
  7.4 39.1 %copy-start = (bf16[2,2,256,256]{3,2,1,0:T(8,128)(2,1)S(1)}, bf16[2,2,256,256]{3,2,1,0:T(8,128)(2,1)}, u32[]{:S(2)}) copy-start(bf16[2,2,256,256]{3,2,1,0:T(8,128)(2,1)} %param.19) | copy-start | bytes 1572868
  7.4 27.7 %all-gather.5.cloned.1.call-start = ((), (), s32[]{:S(2)}) async-start(), calls=%async_computation.1 | async-start | bytes 2621440 | tf_op jit(solution)/shard_map/all_gather | solution.py:67
  8.1 639.0 %all-reduce.34.cloned.1.call-start = ((), (), s32[]{:S(2)}) async-start(), calls=%async_computation.2 | async-start | bytes 4194304 | tf_op jit(solution)/shard_map/psum | solution.py:105
  37.1 7.6 copy-start.12
  37.1 9.0 %copy-start.10 = (f32[512]{0:T(512)S(1)}, f32[512]{0:T(512)}, u32[]{:S(2)}) copy-start(f32[512]{0:T(512)} %param.18) | copy-start | bytes 6148
  41.3 4.7 collective-permute-start
  46.1 2.1 copy-start.11
  56.2 62.4 %copy-start.8 = (bf16[256,4096]{1,0:T(8,128)(2,1)S(1)}, bf16[256,4096]{1,0:T(8,128)(2,1)}, u32[]{:S(2)}) copy-start(bf16[256,4096]{1,0:T(8,128)(2,1)} %all-gather.5.cloned.1.call-done) | copy-start | bytes 6291460
  56.2 62.4 %copy-start.13 = (f32[4096]{0:T(1024)S(1)}, f32[4096]{0:T(1024)}, u32[]{:S(2)}) copy-start(f32[4096]{0:T(1024)} %param.15) | copy-start | bytes 49156
  126.5 620.2 %all-gather.7.cloned.1.call-start = ((), (), s32[]{:S(2)}) async-start(), calls=%async_computation.3 | async-start | bytes 14155776 | tf_op jit(solution)/shard_map/all_gather | solution.py:118
  127.1 660.4 %reduce-scatter.2.cloned.1.call-start = ((), (), s32[]{:S(2)}) async-start(), calls=%async_computation.4 | async-start | bytes 2621440 | tf_op jit(solution)/shard_map/reduce_scatter | solution.py:121
  130.5 126.7 %collective-permute-start.1 = (bf16[2,512,1536]{1,2,0:T(8,128)(2,1)S(1)}, bf16[2,512,1536]{1,2,0:T(8,128)(2,1)S(1)}, u32[]{:S(2)}, u32[]{:S(2)}) collective-permute-start(bf16[2,512,1536]{1,2,0:T(8,128)(2,1)S(1)} %copy.23), channel_id=1, source_target_pairs={{0,4},{4,8},{8,12},{12,16},{16,20},{20,24},{24,28},{28,0},{1,5},{5... | collective-permute-start | bytes 9437192 | tf_op jit(solution)/shard_map/ppermute | solution.py:13
  257.2 206.0 %copy-start.2 = (bf16[2,512,1536]{1,2,0:T(8,128)(2,1)}, bf16[2,512,1536]{1,2,0:T(8,128)(2,1)S(1)}, u32[]{:S(2)}) copy-start(bf16[2,512,1536]{1,2,0:T(8,128)(2,1)S(1)} %collective-permute-done.1) | copy-start | bytes 9437188
  257.2 186.5 %collective-permute-start.2 = (bf16[2,512,1536]{1,2,0:T(8,128)(2,1)S(1)}, bf16[2,512,1536]{1,2,0:T(8,128)(2,1)S(1)}, u32[]{:S(2)}, u32[]{:S(2)}) collective-permute-start(bf16[2,512,1536]{1,2,0:T(8,128)(2,1)S(1)} %collective-permute-done.1), channel_id=1, source_target_pairs={{0,4},{4,8},{8,12},{12,16},{16,20},{20,24},{24,28},{28,0},{1,5},{5... | collective-permute-start | bytes 9437192 | tf_op jit(solution)/shard_map/ppermute | solution.py:13
  257.2 206.0 %collective-permute-start.5 = (bf16[2,512,1536]{1,2,0:T(8,128)(2,1)S(1)}, bf16[2,512,1536]{1,2,0:T(8,128)(2,1)S(1)}, u32[]{:S(2)}, u32[]{:S(2)}) collective-permute-start(bf16[2,512,1536]{1,2,0:T(8,128)(2,1)S(1)} %copy.23), channel_id=1, source_target_pairs={{0,28},{4,0},{8,4},{12,8},{16,12},{20,16},{24,20},{28,24},{1,29},{... | collective-permute-start | bytes 9437192 | tf_op jit(solution)/shard_map/ppermute | solution.py:15
  443.7 200.4 %copy-start.6 = (bf16[2,512,1536]{1,2,0:T(8,128)(2,1)}, bf16[2,512,1536]{1,2,0:T(8,128)(2,1)S(1)}, u32[]{:S(2)}) copy-start(bf16[2,512,1536]{1,2,0:T(8,128)(2,1)S(1)} %collective-permute-done.2) | copy-start | bytes 9437188
  443.7 113.8 %collective-permute-start.3 = (bf16[2,512,1536]{1,2,0:T(8,128)(2,1)S(1)}, bf16[2,512,1536]{1,2,0:T(8,128)(2,1)}, u32[]{:S(2)}, u32[]{:S(2)}) collective-permute-start(bf16[2,512,1536]{1,2,0:T(8,128)(2,1)S(1)} %collective-permute-done.2), channel_id=1, source_target_pairs={{0,4},{4,8},{8,12},{12,16},{16,20},{20,24},{24,28},{28,0},{1,5},{5... | collective-permute-start | bytes 9437192 | tf_op jit(solution)/shard_map/ppermute | solution.py:13
  463.2 7.0 copy-start.4
  463.2 180.9 %collective-permute-start.6 = (bf16[2,512,1536]{1,2,0:T(8,128)(2,1)S(1)}, bf16[2,512,1536]{1,2,0:T(8,128)(2,1)}, u32[]{:S(2)}, u32[]{:S(2)}) collective-permute-start(bf16[2,512,1536]{1,2,0:T(8,128)(2,1)S(1)} %collective-permute-done.5), channel_id=1, source_target_pairs={{0,28},{4,0},{8,4},{12,8},{16,12},{20,16},{24,20},{28,24},{1,29},{... | collective-permute-start | bytes 9437192 | tf_op jit(solution)/shard_map/ppermute | solution.py:15
  557.5 92.8 %collective-permute-start.4 = (bf16[2,512,1536]{1,2,0:T(8,128)(2,1)}, bf16[2,512,1536]{1,2,0:T(8,128)(2,1)}, u32[]{:S(2)}, u32[]{:S(2)}) collective-permute-start(bf16[2,512,1536]{1,2,0:T(8,128)(2,1)} %collective-permute-done.3), channel_id=1, source_target_pairs={{0,4},{4,8},{8,12},{12,16},{16,20},{20,24},{24,28},{28,0},{1,5},{5... | collective-permute-start | bytes 9437192 | tf_op jit(solution)/shard_map/ppermute | solution.py:13
  644.1 62.8 %collective-permute-start.7 = (bf16[2,512,1536]{1,2,0:T(8,128)(2,1)}, bf16[2,512,1536]{1,2,0:T(8,128)(2,1)}, u32[]{:S(2)}, u32[]{:S(2)}) collective-permute-start(bf16[2,512,1536]{1,2,0:T(8,128)(2,1)} %collective-permute-done.6), channel_id=1, source_target_pairs={{0,28},{4,0},{8,4},{12,8},{16,12},{20,16},{24,20},{28,24},{1,29},{... | collective-permute-start | bytes 9437192 | tf_op jit(solution)/shard_map/ppermute | solution.py:15
  650.3 82.9 %copy-start.9 = (bf16[256,4096]{1,0:T(8,128)(2,1)}, bf16[256,4096]{1,0:T(8,128)(2,1)S(1)}, u32[]{:S(2)}) copy-start(bf16[256,4096]{1,0:T(8,128)(2,1)S(1)} %get-tuple-element.129) | copy-start | bytes 6291460
  654.9 3.9 copy-start.7
  658.8 3.0 copy-start.3
  663.7 3.0 copy-start.5
  729.4 3.8 copy-start.14
  746.7 43.0 %copy-start.1 = (bf16[2,2,256,256]{3,2,1,0:T(8,128)(2,1)S(1)}, bf16[2,2,256,256]{3,2,1,0:T(8,128)(2,1)}, u32[]{:S(2)}) copy-start(bf16[2,2,256,256]{3,2,1,0:T(8,128)(2,1)} %param.19) | copy-start | bytes 1572868
Sparse Core Ops, SparseCore 0:
  9.7 25.2 all-gather.4
  126.6 47.7 all-reduce.33
  757.7 29.7 reduce-scatter.1
Sparse Core Ops, SparseCore 1:
  129.0 388.7 all-gather.6
